TPU v7x, 32 devices: a whole 2x2x4 slice. The times are simulated.
32 devices in a mesh: dp: 4 (over y, x), expert: 8 (over z, core).
Axes of the slice: x: 2, y: 2, z: 4, core: 2. Of those that a mesh axis runs over, the one named last changes fastest.
Arguments:
- inputs: bfloat16 [16384, 768], P(('dp', 'expert')), may hold values from -6 to 6
- cotangent: bfloat16 [16384, 768], P(('dp', 'expert')), may hold values from -6 to 6
- lengths: int32 [32], P(('dp', 'expert')), may hold values from 384 to 512, as said below
- routes: int32 [16384, 2], P(('dp', 'expert')), may hold values from 0 to 7, all different within a row; in each aligned block of 512 rows (0 to 511, 512 to 1023, ...) at most 192 rows name the same one
- w_qkv: bfloat16 [768, 2304], P('dp'), may hold values from -0.21875 to 0.21875
- w_attn_out: bfloat16 [768, 768], P('dp'), may hold values from -1.25 to 1.25
- w_router: bfloat16 [768, 8], P('dp'), may hold values from -0.4375 to 0.4375
- gain_attn: bfloat16 [768], P('dp'), may hold values from 0.5 to 1.5
- gain_moe: bfloat16 [768], P('dp'), may hold values from 0.5 to 1.5
- rel_bias: bfloat16 [12, 32], P('dp'), may hold values from -4 to 4
- w_in: bfloat16 [8, 768, 3072], P('expert'), may hold values from -0.21875 to 0.21875
- w_out: bfloat16 [8, 768, 3072], P('expert'), may hold values from -0.109375 to 0.109375
Outputs:
- outputs: bfloat16 [16384, 768], P(('dp', 'expert'))
- d_inputs: bfloat16 [16384, 768], P(('dp', 'expert'))
- grad_qkv: float32 [768, 2304], P('dp')
- grad_attn_out: float32 [768, 768], P('dp')
- grad_router: float32 [768, 8], P('dp')
- grad_gain_attn: float32 [768], P('dp')
- grad_gain_moe: float32 [768], P('dp')
- grad_rel_bias: float32 [12, 32], P('dp')
- grad_w_in: float32 [8, 768, 3072], P('expert', None, 'dp')
- grad_w_out: float32 [8, 768, 3072], P('expert', None, 'dp')
Inputs may be any that keep to these rules, and one draw needn't show every extreme that they name: `lengths`: slots of a sequence at or past its length are padding; some sequence is full and some has the fewest valid tokens. `routes`: a token names two different experts; in the rows of one device no expert is named more than 192 times, a bound that some block reaches.
All inputs are finite; a program needn't handle non-finite values.
Results may differ from a plain program's by a relative error of at most 0.018.
Values may be sent and summed in bfloat16 or wider, within the bound.
A program may use at most 256 MiB of HBM per device.

v0:
```python
import jax
import jax.numpy as jnp
from jax import lax
from jax.sharding import PartitionSpec as P

norm_eps = 1e-06
rel_edges = (19, 21, 24, 27, 31, 35, 40, 46, 52, 59, 67, 77, 87, 99, 113)


def rms_apply(vector, gain_vec):
    return (
        vector * lax.rsqrt(jnp.mean(vector * vector, axis=-1, keepdims=True) + norm_eps) * gain_vec
    )


def bucket_of(distance):
    far_bucket = jnp.full(distance.shape, 16, jnp.int32)
    for edge_value in rel_edges:
        far_bucket = far_bucket + (distance >= edge_value).astype(jnp.int32)
    return jnp.where(distance < 16, distance, far_bucket)


def on_device(
    inputs,
    cotangent,
    lengths,
    routes,
    w_qkv,
    w_attn_out,
    w_router,
    gain_attn,
    gain_moe,
    rel_bias,
    w_in,
    w_out,
):
    w_proj, w_mix, w_gate, gain_one, gain_two, bias_table = (
        lax.all_gather(w_qkv, "dp", axis=0, tiled=True),
        lax.all_gather(w_attn_out, "dp", axis=0, tiled=True),
        lax.all_gather(w_router, "dp", axis=0, tiled=True),
        lax.all_gather(gain_attn, "dp", axis=0, tiled=True),
        lax.all_gather(gain_moe, "dp", axis=0, tiled=True),
        lax.all_gather(rel_bias, "dp", axis=0, tiled=True),
    )
    tok_count, model_width = inputs.shape
    head_count, bucket_count = bias_table.shape
    head_size = model_width // head_count
    top_count = routes.shape[1]
    expert_count = w_gate.shape[1]
    local_count = w_in.shape[0]
    group_count = expert_count // local_count
    capacity = 3 * tok_count * top_count // (2 * expert_count)
    block_rows = min(512, tok_count)
    block_count = tok_count // block_rows
    score_scale = head_size ** (-0.5)
    positions = jnp.arange(tok_count, dtype=jnp.int32)
    valid_mask = (positions < lengths[0]).astype(jnp.float32)
    inputs_wide = inputs.astype(jnp.float32)
    gain_first = gain_one.astype(jnp.float32)
    gain_second = gain_two.astype(jnp.float32)
    normed_attn = rms_apply(inputs_wide, gain_first).astype(jnp.bfloat16)
    proj_qkv = jnp.dot(normed_attn, w_proj, preferred_element_type=jnp.float32).astype(jnp.bfloat16)
    query_heads = proj_qkv[:, :model_width].reshape(tok_count, head_count, head_size)
    key_heads = proj_qkv[:, model_width : 2 * model_width].reshape(tok_count, head_count, head_size)
    value_heads = proj_qkv[:, 2 * model_width :].reshape(tok_count, head_count, head_size)
    bucket_ids = jnp.arange(bucket_count, dtype=jnp.int32)

    def scores_of(row_start):
        distance = (row_start + jnp.arange(block_rows, dtype=jnp.int32))[:, None] - positions[
            None, :
        ]
        allowed = (distance >= 0) & (positions[None, :] < lengths[0])
        one_hot = (bucket_of(jnp.maximum(distance, 0))[:, :, None] == bucket_ids).astype(
            jnp.bfloat16
        )
        bias_term = jnp.einsum(
            "hb,qkb->hqk", bias_table, one_hot, preferred_element_type=jnp.float32
        )
        raw_scores = (
            jnp.einsum("qhd,khd->hqk", query_heads, key_heads, preferred_element_type=jnp.float32)
            * score_scale
            + bias_term
        )
        return (query_heads, one_hot, jnp.where(allowed[None], raw_scores, -1e30))

    def forward_block(block_index):
        row_start = block_index * block_rows
        query_block, one_hot, raw_scores = scores_of(row_start)
        top_score = jnp.max(raw_scores, axis=-1, keepdims=True)
        exp_terms = jnp.exp(raw_scores - top_score)
        row_total = jnp.sum(exp_terms, axis=-1, keepdims=True)
        attn_prob = (exp_terms / row_total).astype(jnp.bfloat16)
        head_out = jnp.einsum(
            "hqk,khd->qhd", attn_prob, value_heads, preferred_element_type=jnp.float32
        )
        return (
            head_out.reshape(block_rows, model_width).astype(jnp.bfloat16),
            top_score[..., 0] + jnp.log(row_total[..., 0]),
        )

    attn_heads, log_totals = lax.map(forward_block, jnp.arange(block_count, dtype=jnp.int32))
    attn_heads = attn_heads.reshape(tok_count, model_width)
    attn_proj = jnp.dot(attn_heads, w_mix, preferred_element_type=jnp.float32)
    hidden = inputs_wide + valid_mask[:, None] * attn_proj
    normed_moe = rms_apply(hidden, gain_second).astype(jnp.bfloat16)
    logits = jnp.dot(normed_moe, w_gate, preferred_element_type=jnp.float32)
    expert_ids = jnp.arange(expert_count, dtype=jnp.int32)
    chosen_mask = (routes[:, :, None] == expert_ids).astype(jnp.float32)
    chosen = jnp.sum(logits[:, None, :] * chosen_mask, axis=-1)
    gate_pair = jax.nn.softmax(chosen, axis=-1)
    gate_used = gate_pair * valid_mask[:, None]
    flat_routes = routes.reshape(-1)
    flat_valid = jnp.broadcast_to(valid_mask[:, None], routes.shape).reshape(-1) > 0
    route_hot = ((flat_routes[:, None] == expert_ids) & flat_valid[:, None]).astype(jnp.int32)
    rank_in = jnp.sum((jnp.cumsum(route_hot, axis=0) - route_hot) * route_hot, axis=1)
    slot_index = jnp.where(flat_valid, flat_routes * capacity + rank_in, expert_count * capacity)
    route_ids = jnp.arange(tok_count * top_count, dtype=jnp.int32)
    source = jnp.zeros((expert_count * capacity + 1,), jnp.int32).at[slot_index].set(route_ids)[:-1]
    filled = jnp.zeros((expert_count * capacity + 1,), jnp.bfloat16).at[slot_index].set(1)[:-1]
    send_rows = (normed_moe[source // top_count] * filled[:, None]).reshape(
        group_count, local_count, capacity, model_width
    )
    recv_rows = lax.all_to_all(send_rows, "expert", split_axis=0, concat_axis=0, tiled=True)
    pre_act = jnp.einsum("nekd,edf->nekf", recv_rows, w_in, preferred_element_type=jnp.float32)
    activation = jax.nn.gelu(pre_act).astype(jnp.bfloat16)
    expert_out = jnp.einsum(
        "nekf,edf->nekd", activation, w_out, preferred_element_type=jnp.float32
    ).astype(jnp.bfloat16)
    returned = lax.all_to_all(expert_out, "expert", split_axis=0, concat_axis=0, tiled=True)
    results = (returned, recv_rows, pre_act)
    returned = results[0]
    kept_rows = results[1]
    out_table = jnp.concatenate(
        [
            returned.reshape(expert_count * capacity, model_width),
            jnp.zeros((1, model_width), jnp.bfloat16),
        ],
        axis=0,
    )
    picked = out_table[slot_index].reshape(tok_count, top_count, model_width).astype(jnp.float32)
    moe_out = jnp.sum(gate_used[:, :, None] * picked, axis=1)
    outputs = (valid_mask[:, None] * (hidden + moe_out)).astype(jnp.bfloat16)
    grad_out = cotangent.astype(jnp.float32) * valid_mask[:, None]
    d_gate = jnp.sum(grad_out[:, None, :] * picked, axis=-1) * valid_mask[:, None]
    d_chosen = gate_pair * (d_gate - jnp.sum(gate_pair * d_gate, axis=-1, keepdims=True))
    d_logits = jnp.sum(d_chosen[:, :, None] * chosen_mask, axis=1).astype(jnp.bfloat16)
    grad_router = jnp.dot(normed_moe.T, d_logits, preferred_element_type=jnp.float32)
    d_normed = jnp.dot(d_logits, w_gate.T, preferred_element_type=jnp.float32)
    route_weight = gate_used.reshape(-1)
    d_send = (
        grad_out[source // top_count] * (route_weight[source] * filled.astype(jnp.float32))[:, None]
    ).astype(jnp.bfloat16)
    d_send = d_send.reshape(group_count, local_count, capacity, model_width)
    d_recv = lax.all_to_all(d_send, "expert", split_axis=0, concat_axis=0, tiled=True)
    pre_act = results[2]
    act_full, gelu_back = jax.vjp(jax.nn.gelu, pre_act)
    activation = act_full.astype(jnp.bfloat16)
    d_act = jnp.einsum("nekd,edf->nekf", d_recv, w_out, preferred_element_type=jnp.float32)
    d_pre = gelu_back(d_act)[0].astype(jnp.bfloat16)
    full_w_out = jnp.einsum(
        "nekd,nekf->edf", d_recv, activation, preferred_element_type=jnp.float32
    )
    full_w_in = jnp.einsum("nekd,nekf->edf", kept_rows, d_pre, preferred_element_type=jnp.float32)
    d_rows = jnp.einsum("nekf,edf->nekd", d_pre, w_in, preferred_element_type=jnp.float32).astype(
        jnp.bfloat16
    )
    d_returned = lax.all_to_all(d_rows, "expert", split_axis=0, concat_axis=0, tiled=True)
    grad_w_in, grad_w_out = (
        lax.psum_scatter(
            full_w_in.astype(jnp.bfloat16), "dp", scatter_dimension=2, tiled=True
        ).astype(jnp.float32),
        lax.psum_scatter(
            full_w_out.astype(jnp.bfloat16), "dp", scatter_dimension=2, tiled=True
        ).astype(jnp.float32),
    )
    d_table = jnp.concatenate(
        [
            d_returned.reshape(expert_count * capacity, model_width),
            jnp.zeros((1, model_width), jnp.bfloat16),
        ],
        axis=0,
    )
    d_normed = d_normed + jnp.sum(
        d_table[slot_index].reshape(tok_count, top_count, model_width).astype(jnp.float32), axis=1
    )
    second_val, second_back = jax.vjp(rms_apply, hidden, gain_second)
    d_hidden_norm, grad_gain_moe = second_back(d_normed)
    d_hidden = grad_out + d_hidden_norm
    d_attn_proj = (d_hidden * valid_mask[:, None]).astype(jnp.bfloat16)
    grad_attn_out = jnp.dot(attn_heads.T, d_attn_proj, preferred_element_type=jnp.float32)
    d_heads = (
        jnp.dot(d_attn_proj, w_mix.T, preferred_element_type=jnp.float32)
        .astype(jnp.bfloat16)
        .reshape(tok_count, head_count, head_size)
    )

    def backward_block(carry, block_index):
        d_keys, d_values, d_bias = carry
        row_start = block_index * block_rows
        query_block, one_hot, raw_scores = scores_of(row_start)
        attn_full = jnp.exp(raw_scores - log_totals[block_index][..., None])
        attn_prob = attn_full.astype(jnp.bfloat16)
        d_values = d_values + jnp.einsum(
            "hqk,qhd->khd", attn_prob, d_heads, preferred_element_type=jnp.float32
        )
        d_prob = jnp.einsum(
            "qhd,khd->hqk", d_heads, value_heads, preferred_element_type=jnp.float32
        )
        d_scores = (
            attn_full * (d_prob - jnp.sum(attn_full * d_prob, axis=-1, keepdims=True))
        ).astype(jnp.bfloat16)
        d_query = (
            jnp.einsum("hqk,khd->qhd", d_scores, key_heads, preferred_element_type=jnp.float32)
            * score_scale
        )
        d_keys = (
            d_keys
            + jnp.einsum("hqk,qhd->khd", d_scores, query_block, preferred_element_type=jnp.float32)
            * score_scale
        )
        d_bias = d_bias + jnp.einsum(
            "hqk,qkb->hb", d_scores, one_hot, preferred_element_type=jnp.float32
        )
        return ((d_keys, d_values, d_bias), d_query)

    start_carry = (
        jnp.zeros((tok_count, head_count, head_size), jnp.float32),
        jnp.zeros((tok_count, head_count, head_size), jnp.float32),
        jnp.zeros((head_count, bucket_count), jnp.float32),
    )
    final_carry, d_queries = lax.scan(
        backward_block, start_carry, jnp.arange(block_count, dtype=jnp.int32)
    )
    d_keys, d_values, grad_rel_bias = final_carry
    d_qkv = jnp.concatenate(
        [
            d_queries.reshape(tok_count, model_width),
            d_keys.reshape(tok_count, model_width),
            d_values.reshape(tok_count, model_width),
        ],
        axis=1,
    ).astype(jnp.bfloat16)
    grad_qkv = jnp.dot(normed_attn.T, d_qkv, preferred_element_type=jnp.float32)
    d_normed_attn = jnp.dot(d_qkv, w_proj.T, preferred_element_type=jnp.float32)
    first_val, first_back = jax.vjp(rms_apply, inputs_wide, gain_first)
    d_norm_in, grad_gain_attn = first_back(d_normed_attn)
    d_inputs = (d_hidden + d_norm_in).astype(jnp.bfloat16)
    summed = lax.psum(
        (grad_qkv, grad_attn_out, grad_router, grad_gain_attn, grad_gain_moe, grad_rel_bias),
        "expert",
    )
    shares = (
        lax.psum_scatter(
            summed[0].astype(jnp.bfloat16), "dp", scatter_dimension=0, tiled=True
        ).astype(jnp.float32),
        lax.psum_scatter(
            summed[1].astype(jnp.bfloat16), "dp", scatter_dimension=0, tiled=True
        ).astype(jnp.float32),
        lax.psum_scatter(
            summed[2].astype(jnp.bfloat16), "dp", scatter_dimension=0, tiled=True
        ).astype(jnp.float32),
        lax.psum_scatter(
            summed[3].astype(jnp.bfloat16), "dp", scatter_dimension=0, tiled=True
        ).astype(jnp.float32),
        lax.psum_scatter(
            summed[4].astype(jnp.bfloat16), "dp", scatter_dimension=0, tiled=True
        ).astype(jnp.float32),
        lax.psum_scatter(
            summed[5].astype(jnp.bfloat16), "dp", scatter_dimension=0, tiled=True
        ).astype(jnp.float32),
    )
    return (
        outputs,
        d_inputs,
        shares[0],
        shares[1],
        shares[2],
        shares[3],
        shares[4],
        shares[5],
        grad_w_in,
        grad_w_out,
    )


def solution(mesh):
    placed = (
        P(("dp", "expert"), None),
        P(("dp", "expert"), None),
        P(("dp", "expert")),
        P(("dp", "expert"), None),
        P("dp", None),
        P("dp", None),
        P("dp", None),
        P("dp"),
        P("dp"),
        P("dp", None),
        P("expert", None, None),
        P("expert", None, None),
    )
    return jax.shard_map(
        on_device,
        mesh=mesh,
        in_specs=placed,
        out_specs=(
            P(("dp", "expert"), None),
            P(("dp", "expert"), None),
            P("dp", None),
            P("dp", None),
            P("dp", None),
            P("dp"),
            P("dp"),
            P("dp", None),
            P("expert", None, "dp"),
            P("expert", None, "dp"),
        ),
        check_vma=False,
    )
```

profile of v0, /device:TPU:0, one launch (start us, length us, event | category | flops | bytes accessed | tf_op | source)
XLA Modules:
  0.0 836.9 jit_solution(11482958832264062407)
XLA Ops:
  14.5 11.6 %all-reduce.9 = (bf16[768]{0:T(1024)(128)(2,1)S(1)}, bf16[768]{0:T(1024)(128)(2,1)S(1)}) all-reduce(bf16[768]{0:T(1024)(128)(2,1)S(1)} %dynamic-update-slice, bf16[768]{0:T(1024)(128)(2,1)S(1)} %dynamic-update-slice.1), channel_id=1, replica_groups=mesh['dp'=4,'expert'=8] {'dp'}, use_global_device_ids=true, to_apply=%add.2 | all-reduce | flops 1536 | bytes 6144
  49.2 8.5 %fusion.1 = f32[512,512,12]{0,2,1:T(8,128)} fusion(bf16[12,32,1]{1,0,2:T(8,128)(2,1)S(1)} %reshape.597, s32[512,512]{0,1:T(8,128)S(1)} %compare_select_fusion), kind=kOutput, calls=%fused_computation.9 | convolution fusion | flops 209715200 | bytes 13632256 | tf_op jit(solution)/shard_map/while/body/eval_jaxpr/hb,qkb->hqk/dot_general | solution.py:76
  66.9 15.6 %fusion.132 = (f32[12,512]{1,0:T(8,128)S(1)}, f32[12,512,512]{1,2,0:T(8,128)S(1)}) fusion(f32[512,512,12]{0,2,1:T(8,128)} %fusion.1, bf16[512,12,64]{0,2,1:T(8,128)(2,1)S(1)} %bitcast.217, bf16[512,12,64]{0,2,1:T(8,128)(2,1)S(1)} %bitcast.212, pred[512,512]{0,1:T(8,128)(4,1)S(1)} %fusion.93), kind=kOutput, calls=%fused_computation.192 | convolution fusion | flops 415229952 | bytes 27025408 | tf_op jit(solution)/shard_map/while/body/eval_jaxpr/qhd,khd->hqk/dot_general | solution.py:80
  109.9 8.1 all-gather.1
  134.7 29.9 %all-to-all-done = bf16[8,1,192,768]{3,2,1,0:T(8,128)(2,1)} async-done(((bf16[8,1,192,768]{3,2,1,0:T(8,128)(2,1)}), bf16[8,1,192,768]{3,2,1,0:T(8,128)(2,1)}, u32[]{:S(2)}, u32[]{:S(2)}) %all-to-all-start) | async-done | bytes 2359328 | tf_op jit(solution)/shard_map/all_to_all | solution.py:123
  169.4 13.7 %fusion.38 = f32[8,192,3072]{2,1,0:T(8,128)} fusion(bf16[1,768,3072]{2,1,0:T(8,128)(2,1)} %param.22, bf16[8,1,192,768]{3,2,1,0:T(8,128)(2,1)} %all-to-all-done), kind=kOutput, calls=%fused_computation.54 | convolution fusion | flops 7247757312 | bytes 25952256 | tf_op jit(solution)/shard_map/nekd,edf->nekf/dot_general | solution.py:124
  183.1 17.4 %convert_bitcast_fusion.1 = bf16[8,1,192,768]{3,2,1,0:T(8,128)(2,1)} fusion(bf16[1,768,3072]{2,1,0:T(8,128)(2,1)} %param.23, f32[8,192,3072]{2,1,0:T(8,128)} %fusion.38), kind=kOutput, calls=%fused_computation.76 | convolution fusion | flops 7291404288 | bytes 25952256 | tf_op jit(solution)/shard_map/nekf,edf->nekd/dot_general | solution.py:126
  200.5 23.6 %all-to-all-done.2 = bf16[8,1,192,768]{3,2,1,0:T(8,128)(2,1)} async-done(((bf16[8,1,192,768]{3,2,1,0:T(8,128)(2,1)}), bf16[8,1,192,768]{3,2,1,0:T(8,128)(2,1)}, u32[]{:S(2)}, u32[]{:S(2)}) %all-to-all-start.2) | async-done | bytes 2359328 | tf_op jit(solution)/shard_map/all_to_all | solution.py:154
  228.6 22.0 %fusion.8 = bf16[8,1,192,3072]{3,2,0,1:T(8,128)(2,1)S(1)} fusion(f32[8,192,3072]{2,1,0:T(8,128)} %fusion.38, bf16[1,768,3072]{2,1,0:T(8,128)(2,1)} %param.23, bf16[8,1,192,768]{3,2,1,0:T(8,128)(2,1)} %all-to-all-done.2), kind=kOutput, calls=%fused_computation.18 | convolution fusion | flops 7342129152 | bytes 35389440 | tf_op jit(solution)/shard_map/nekd,edf->nekf/dot_general | solution.py:158
  254.3 11.1 %convert_bitcast_fusion = bf16[8,1,192,768]{3,2,1,0:T(8,128)(2,1)} fusion(bf16[1,768,3072]{2,1,0:T(8,128)(2,1)} %param.22, bf16[8,1,192,3072]{3,2,0,1:T(8,128)(2,1)S(1)} %fusion.8), kind=kOutput, calls=%fused_computation.75 | convolution fusion | flops 7248936960 | bytes 16515072 | tf_op jit(solution)/shard_map/nekf,edf->nekd/dot_general | solution.py:164
  265.4 17.9 %all-to-all-done.1 = bf16[8,1,192,768]{3,2,1,0:T(8,128)(2,1)} async-done(((bf16[8,1,192,768]{3,2,1,0:T(8,128)(2,1)}), bf16[8,1,192,768]{3,2,1,0:T(8,128)(2,1)}, u32[]{:S(2)}, u32[]{:S(2)}) %all-to-all-start.1) | async-done | bytes 2359328 | tf_op jit(solution)/shard_map/all_to_all | solution.py:129
  291.0 7.7 gather_fusion.1
  303.7 9.4 %multiply_reduce_fusion.1 = (f32[512,2]{1,0:T(8,128)S(1)}, f32[512,768]{1,0:T(8,128)}) fusion(f32[512,2,768]{2,1,0:T(2,128)} %reshape.522, f32[512,768]{1,0:T(8,128)S(1)} %convert_multiply_fusion.4, f32[512,2]{1,0:T(8,128)S(1)} %copy.127), kind=kLoop, calls=%fused_computation.60 | loop fusion | flops 2751488 | bytes 6299648 | tf_op jit(solution)/shard_map/reduce_sum | solution.py:144
  313.4 28.9 %all-to-all-done.3 = bf16[8,1,192,768]{3,2,1,0:T(8,128)(2,1)} async-done(((bf16[8,1,192,768]{3,2,1,0:T(8,128)(2,1)}), bf16[8,1,192,768]{3,2,1,0:T(8,128)(2,1)}, u32[]{:S(2)}, u32[]{:S(2)}) %all-to-all-start.3) | async-done | bytes 2359328 | tf_op jit(solution)/shard_map/all_to_all | solution.py:167
  375.4 7.7 multiply_reduce_fusion
  388.5 10.4 %fusion.73 = f32[12,32]{1,0:T(8,128)S(1)} fusion(s32[512,512]{0,1:T(8,128)} %copy-done.12, bf16[12,512,512]{1,2,0:T(8,128)(2,1)} %multiply_convert_fusion), kind=kOutput, calls=%fused_computation.100 | convolution fusion | flops 209715200 | bytes 7341568 | tf_op jit(solution)/shard_map/while/body/eval_jaxpr/hqk,qkb->hb/dot_general | solution.py:221
  414.0 188.6 %all-reduce.11 = (bf16[768,2304]{1,0:T(8,128)(2,1)}, bf16[768,768]{1,0:T(8,128)(2,1)}, bf16[768,8]{0,1:T(8,128)(2,1)S(1)}, bf16[768]{0:T(1024)(128)(2,1)S(1)}, b...) all-reduce(f32[768,2304]{1,0:T(8,128)} %fusion.94, ...), channel_id=1, replica_groups=mesh['dp'=4,'expert'=8] {'expert'}, use_global_device_ids=true, to_apply=%region_20.21 | all-reduce | flops 2367360 | bytes 14204160 | tf_op jit(solution)/shard_map/psum | solution.py:248
  604.1 14.3 %fusion.43 = bf16[1,768,3072]{2,1,0:T(8,128)(2,1)} fusion(f32[8,192,3072]{2,1,0:T(8,128)} %fusion.38, bf16[8,1,192,768]{3,2,1,0:T(8,128)(2,1)} %all-to-all-done.2), kind=kOutput, calls=%fused_computation.58 | convolution fusion | flops 7292583936 | bytes 25952256 | tf_op jit(solution)/shard_map/nekd,nekf->edf/dot_general | solution.py:160
  618.5 12.5 %fusion.40 = bf16[1,768,3072]{2,1,0:T(8,128)(2,1)} fusion(bf16[8,1,192,3072]{3,2,0,1:T(8,128)(2,1)} %copy-done.38, bf16[8,1,192,768]{3,2,1,0:T(8,128)(2,1)} %all-to-all-done), kind=kOutput, calls=%fused_computation.57 | convolution fusion | flops 7250116608 | bytes 16515072 | tf_op jit(solution)/shard_map/nekd,nekf->edf/dot_general | solution.py:163
  633.1 9.6 %all-reduce.8 = (bf16[768]{0:T(1024)(128)(2,1)S(1)}, bf16[768]{0:T(1024)(128)(2,1)S(1)}, bf16[12,32]{1,0:T(8,128)(2,1)S(1)}) all-reduce(bf16[768]{0:T(1024)(128)(2,1)S(1)} %get-tuple-element.77, bf16[768]{0:T(1024)(128)(2,1)S(1)} %get-tuple-element.78, ...), channel_id=5, replica_groups=mesh['dp'=4,'expert'=8] {'dp'}, use_global_device_ids=true, to_apply=%region_28.29.clone | all-reduce | flops 1920 | bytes 7680
  648.8 8.6 %reduce-scatter.10.cloned.1.call-done = bf16[192,768]{1,0:T(8,128)(2,1)} async-done(((bf16[768,768]{1,0:T(8,128)(2,1)}), bf16[192,768]{1,0:T(8,128)(2,1)}) %reduce-scatter.10.cloned.1.call-update) | async-done | bytes 294928 | tf_op jit(solution)/shard_map/reduce_scatter | solution.py:256
  659.2 58.0 %reduce-scatter.14.cloned.1.call-done = bf16[1,768,768]{2,1,0:T(8,128)(2,1)} async-done(((bf16[1,768,3072]{2,1,0:T(8,128)(2,1)}), bf16[1,768,768]{2,1,0:T(8,128)(2,1)}) %reduce-scatter.14.cloned.1.call-update) | async-done | bytes 1179664 | tf_op jit(solution)/shard_map/reduce_scatter | solution.py:172
  720.1 57.0 %reduce-scatter.12.cloned.1.call-done = bf16[1,768,768]{2,1,0:T(8,128)(2,1)} async-done(((bf16[1,768,3072]{2,1,0:T(8,128)(2,1)}), bf16[1,768,768]{2,1,0:T(8,128)(2,1)}) %reduce-scatter.12.cloned.1.call-update) | async-done | bytes 1179664 | tf_op jit(solution)/shard_map/reduce_scatter | solution.py:169
  779.9 47.4 %reduce-scatter.8.cloned.1.call-done = bf16[192,2304]{1,0:T(8,128)(2,1)} async-done(((bf16[768,2304]{1,0:T(8,128)(2,1)}), bf16[192,2304]{1,0:T(8,128)(2,1)}) %reduce-scatter.8.cloned.1.call-update) | async-done | bytes 884752 | tf_op jit(solution)/shard_map/reduce_scatter | solution.py:253
  (214 shorter events, 179.5 us)
Async XLA Ops:
  7.2 18.8 %copy-start.33 = (bf16[3,32]{1,0:T(4,128)(2,1)S(1)}, bf16[3,32]{1,0:T(4,128)(2,1)}, u32[]{:S(2)}) copy-start(bf16[3,32]{1,0:T(4,128)(2,1)} %param.21) | copy-start | bytes 580
  7.2 52.6 %all-gather.5.cloned.1.call-start = ((), (), s32[]{:S(2)}) async-start(), calls=%async_computation.9 | async-start | bytes 4423680 | tf_op jit(solution)/shard_map/all_gather | solution.py:38
  8.0 86.6 %all-gather.7.cloned.1.call-start = ((), (), s32[]{:S(2)}) async-start(), calls=%async_computation.10 | async-start | bytes 1474560 | tf_op jit(solution)/shard_map/all_gather | solution.py:39
  12.4 45.4 %copy-start.12 = (s32[512,512]{0,1:T(8,128)}, s32[512,512]{0,1:T(8,128)S(1)}, u32[]{:S(2)}) copy-start(s32[512,512]{0,1:T(8,128)S(1)} %compare_select_fusion) | copy-start | bytes 3145732
  12.7 20.7 %copy-start.23 = (f32[512]{0:T(512)}, f32[512]{0:T(512)S(1)}, u32[]{:S(2)}) copy-start(f32[512]{0:T(512)S(1)} %fusion.67) | copy-start | bytes 6148
  12.7 47.1 %copy-start.29 = (f32[512]{0:T(512)}, f32[512]{0:T(512)S(1)}, u32[]{:S(2)}) copy-start(f32[512]{0:T(512)S(1)} %fusion.115) | copy-start | bytes 6148
  26.0 33.8 %copy-start.25 = (f32[768]{0:T(1024)}, f32[768]{0:T(1024)S(1)}, u32[]{:S(2)}) copy-start(f32[768]{0:T(1024)S(1)} %convert_element_type.378) | copy-start | bytes 9220
  65.2 17.3 %copy-start.6 = (bf16[512,768]{0,1:T(8,128)(2,1)}, bf16[512,768]{0,1:T(8,128)(2,1)S(1)}, u32[]{:S(2)}) copy-start(bf16[512,768]{0,1:T(8,128)(2,1)S(1)} %copy.123) | copy-start | bytes 2359300
  66.9 15.6 %copy-start.10 = (bf16[512,768]{0,1:T(8,128)(2,1)}, bf16[512,768]{0,1:T(8,128)(2,1)S(1)}, u32[]{:S(2)}) copy-start(bf16[512,768]{0,1:T(8,128)(2,1)S(1)} %copy.122) | copy-start | bytes 2359300
  105.1 13.0 %copy-start.17 = (bf16[512,768]{1,0:T(8,128)(2,1)S(1)}, bf16[512,768]{1,0:T(8,128)(2,1)}, u32[]{:S(2)}) copy-start(bf16[512,768]{1,0:T(8,128)(2,1)} %param.13) | copy-start | bytes 2359300
  105.1 59.5 %all-to-all-start = ((bf16[8,1,192,768]{3,2,1,0:T(8,128)(2,1)}), bf16[8,1,192,768]{3,2,1,0:T(8,128)(2,1)}, u32[]{:S(2)}, u32[]{:S(2)}) async-start(bf16[8,1,192,768]{3,2,1,0:T(8,128)(2,1)} %broadcast_multiply_fusion), calls=%async_computation | async-start | bytes 4718592 | tf_op jit(solution)/shard_map/all_to_all | solution.py:123
  164.6 59.5 %all-to-all-start.2 = ((bf16[8,1,192,768]{3,2,1,0:T(8,128)(2,1)}), bf16[8,1,192,768]{3,2,1,0:T(8,128)(2,1)}, u32[]{:S(2)}, u32[]{:S(2)}) async-start(bf16[8,1,192,768]{3,2,1,0:T(8,128)(2,1)} %multiply_convert_fusion.1), calls=%async_computation.2 | async-start | bytes 4718592 | tf_op jit(solution)/shard_map/all_to_all | solution.py:154
  224.1 59.2 %all-to-all-start.1 = ((bf16[8,1,192,768]{3,2,1,0:T(8,128)(2,1)}), bf16[8,1,192,768]{3,2,1,0:T(8,128)(2,1)}, u32[]{:S(2)}, u32[]{:S(2)}) async-start(bf16[8,1,192,768]{3,2,1,0:T(8,128)(2,1)} %convert_bitcast_fusion.1), calls=%async_computation.1 | async-start | bytes 4718592 | tf_op jit(solution)/shard_map/all_to_all | solution.py:129
  265.4 22.3 %copy-start.28 = (s32[1024,1]{0,1:T(1,128)S(1)}, s32[1024,1]{0,1:T(1,128)}, u32[]{:S(2)}) copy-start(s32[1024,1]{0,1:T(1,128)} %copy-done.27) | copy-start | bytes 12292
  283.3 59.0 %all-to-all-start.3 = ((bf16[8,1,192,768]{3,2,1,0:T(8,128)(2,1)}), bf16[8,1,192,768]{3,2,1,0:T(8,128)(2,1)}, u32[]{:S(2)}, u32[]{:S(2)}) async-start(bf16[8,1,192,768]{3,2,1,0:T(8,128)(2,1)} %convert_bitcast_fusion), calls=%async_computation.3 | async-start | bytes 4718592 | tf_op jit(solution)/shard_map/all_to_all | solution.py:167
  287.7 359.7 %reduce-scatter.16.cloned.1.call-start = ((), (), s32[]{:S(2)}) async-start(), calls=%async_computation.15 | async-start | bytes 245760
  367.8 15.4 %slice-start = ((s8[12582912]{0:T(1024)(128)(4,1)}), s8[4194304]{0:T(1024)(128)(4,1)S(1)}, s32[]{:S(2)}) async-start(s8[12582912]{0:T(1024)(128)(4,1)} %bitcast.209), calls=%async_computation.16 | async-start | bytes 8388608
  367.8 15.4 %slice-start.1 = ((s8[12582912]{0:T(1024)(128)(4,1)}), s8[4194304]{0:T(1024)(128)(4,1)S(1)}, s32[]{:S(2)}) async-start(s8[12582912]{0:T(1024)(128)(4,1)} %bitcast.209), calls=%async_computation.17 | async-start | bytes 8388608
  603.5 53.9 %reduce-scatter.10.cloned.1.call-start = ((), (), s32[]{:S(2)}) async-start(), calls=%async_computation.12 | async-start | bytes 1474560 | tf_op jit(solution)/shard_map/reduce_scatter | solution.py:256
  604.1 113.2 %reduce-scatter.14.cloned.1.call-start = ((), (), s32[]{:S(2)}) async-start(), calls=%async_computation.14 | async-start | bytes 5898240 | tf_op jit(solution)/shard_map/reduce_scatter | solution.py:172
  618.5 158.6 %reduce-scatter.12.cloned.1.call-start = ((), (), s32[]{:S(2)}) async-start(), calls=%async_computation.13 | async-start | bytes 5898240 | tf_op jit(solution)/shard_map/reduce_scatter | solution.py:169
  631.0 13.6 %copy-start.24 = (f32[512]{0:T(512)S(1)}, f32[512]{0:T(512)}, u32[]{:S(2)}) copy-start(f32[512]{0:T(512)} %copy-done.23) | copy-start | bytes 6148
  631.0 13.6 %copy-start.3 = (f32[512,768]{1,0:T(8,128)S(1)}, f32[512,768]{1,0:T(8,128)}, u32[]{:S(2)}) copy-start(f32[512,768]{1,0:T(8,128)} %copy-done.2) | copy-start | bytes 4718596
  631.1 196.3 %reduce-scatter.8.cloned.1.call-start = ((), (), s32[]{:S(2)}) async-start(), calls=%async_computation.11 | async-start | bytes 4423680 | tf_op jit(solution)/shard_map/reduce_scatter | solution.py:253
  (29 other events, 121.2 us)
Sparse Core Ops, SparseCore 0:
  9.9 49.8 all-gather.4
  61.6 27.5 all-gather.6
  603.6 21.6 reduce-scatter.15
  628.7 28.6 reduce-scatter.9
  660.3 56.9 reduce-scatter.13
  720.1 56.9 reduce-scatter.11
  780.2 47.1 reduce-scatter.7
where the time goes:
time: 844 us; the launch traced here: 837 us
  waiting for transfers between devices  276 us (33%)
  blocking collectives  225 us (27%)
  matrix products  174 us (21%)
  local copies, waits for them, and re-layouts  75.8 us (9%)
  other arithmetic  49.6 us (6%)
  starting transfers between devices  18.8 us (2%)
  between operations  17.8 us (2%)
    psum x1, blocking collectives, on_device(): lax.psum((grad_qkv, grad_attn_out, grad_router, grad_gain_attn, grad_gain...  189 us
    reduce_scatter x1, waiting for transfers between devices, on_device(): lax.psum_scatter(full_w_out.astype(jnp.bfloat16), 'dp', scatter_dimension...  58 us
    reduce_scatter x1, waiting for transfers between devices, on_device(): lax.psum_scatter(full_w_in.astype(jnp.bfloat16), 'dp', scatter_dimension=...  57 us
    reduce_scatter x1, waiting for transfers between devices, on_device(): lax.psum_scatter(summed[0].astype(jnp.bfloat16), 'dp', scatter_dimension=...  47.4 us
    all_to_all x1, waiting for transfers between devices, on_device(): lax.all_to_all(send_rows, 'expert', split_axis=0, concat_axis=0, tiled=True)  29.9 us
    all_to_all x1, waiting for transfers between devices, on_device(): lax.all_to_all(d_rows, 'expert', split_axis=0, concat_axis=0, tiled=True)  28.9 us
    all_to_all x1, waiting for transfers between devices, on_device(): lax.all_to_all(d_send, 'expert', split_axis=0, concat_axis=0, tiled=True)  23.6 us
    dot_general x1, matrix products, on_device(): jnp.einsum('nekd,edf->nekf', d_recv, w_out, preferred_element_type=jnp.fl...  22 us
  transfers between devices with their start and end apart: 11, of which 9 were waited for; matrix products, arithmetic and copies ran while one was open for 25% of the time, Pallas kernels for 0%

commit v1 on v0

--- a/solution.py
+++ b/solution.py
@@ -5,6 +5,18 @@
 
 norm_eps = 1e-06
 rel_edges = (19, 21, 24, 27, 31, 35, 40, 46, 52, 59, 67, 77, 87, 99, 113)
+
+
+def split_up(array, dim, size):
+    shape = array.shape
+    tiles = array.reshape(*shape[:dim], size, shape[dim] // size, *shape[dim + 1 :])
+    return jnp.moveaxis(tiles, dim, 0)
+
+
+def laid_out(pieces, dim):
+    pieces = jnp.moveaxis(pieces, 0, dim)
+    lengths = pieces.shape
+    return pieces.reshape(*lengths[:dim], lengths[dim] * lengths[dim + 1], *lengths[dim + 2 :])
 
 
 def rms_apply(vector, gain_vec):
@@ -164,7 +176,14 @@
     d_rows = jnp.einsum("nekf,edf->nekd", d_pre, w_in, preferred_element_type=jnp.float32).astype(
         jnp.bfloat16
     )
-    d_returned = lax.all_to_all(d_rows, "expert", split_axis=0, concat_axis=0, tiled=True)
+    size, position = (lax.axis_size("expert"), lax.axis_index("expert"))
+    parts = split_up(d_rows, 0, size)
+    outs = [parts[position]]
+    for hop in range(1, size):
+        sent = parts[position ^ hop]
+        outs.append(lax.ppermute(sent, "expert", [(i, i ^ hop) for i in range(size)]))
+    parts = jnp.stack(outs)[position ^ jnp.arange(size)]
+    d_returned = laid_out(parts, 0)
     grad_w_in, grad_w_out = (
         lax.psum_scatter(
             full_w_in.astype(jnp.bfloat16), "dp", scatter_dimension=2, tiled=True

time: 844 us -> 876 us (1.038)
  waiting for transfers between devices: 276 us -> 286 us
  local copies, waits for them, and re-layouts: 75.8 us -> 85.6 us
    ppermute x0 -> x7, waiting for transfers between devices: none -> 57.1 us  [on_device(): lax.ppermute(sent, 'expert', [(i, i ^ hop) for i in range(size)])]
    all_to_all x1 -> x0, waiting for transfers between devices: 28.9 us -> none  [on_device(): lax.all_to_all(d_rows, 'expert', split_axis=0, concat_axis=0, tiled=True)]
    all_to_all x1, waiting for transfers between devices: 17.9 us -> 0.01 us  [on_device(): lax.all_to_all(expert_out, 'expert', split_axis=0, concat_axis=0, tiled=T...]
    ppermute x0 -> x7, starting transfers between devices: none -> 9.2 us  [on_device(): lax.ppermute(sent, 'expert', [(i, i ^ hop) for i in range(size)])]
  transfers between devices with their start and end apart: 11 -> 17, of which waited for: 9 -> 10; matrix products, arithmetic and copies ran while one was open for 25% -> 25% of each run, Pallas kernels for 0% -> 0%
where the time goes in v1:
time: 876 us; the launch traced here: 868 us
  waiting for transfers between devices  286 us (33%)
  blocking collectives  225 us (26%)
  matrix products  179 us (20%)
  local copies, waits for them, and re-layouts  85.6 us (10%)
  other arithmetic  51.1 us (6%)
  starting transfers between devices  23.1 us (3%)
  between operations  18 us (2%)
    psum x1, blocking collectives, on_device(): lax.psum((grad_qkv, grad_attn_out, grad_router, grad_gain_attn, grad_gain...  189 us
    reduce_scatter x1, waiting for transfers between devices, on_device(): lax.psum_scatter(full_w_out.astype(jnp.bfloat16), 'dp', scatter_dimension...  58 us
    ppermute x7, waiting for transfers between devices, on_device(): lax.ppermute(sent, 'expert', [(i, i ^ hop) for i in range(size)])  57.1 us
    reduce_scatter x1, waiting for transfers between devices, on_device(): lax.psum_scatter(full_w_in.astype(jnp.bfloat16), 'dp', scatter_dimension=...  57 us
    reduce_scatter x1, waiting for transfers between devices, on_device(): lax.psum_scatter(summed[0].astype(jnp.bfloat16), 'dp', scatter_dimension=...  47.4 us
    all_to_all x1, waiting for transfers between devices, on_device(): lax.all_to_all(send_rows, 'expert', split_axis=0, concat_axis=0, tiled=True)  30 us
    all_to_all x1, waiting for transfers between devices, on_device(): lax.all_to_all(d_send, 'expert', split_axis=0, concat_axis=0, tiled=True)  23.6 us
    dot_general x1, matrix products, on_device(): jnp.einsum('nekd,edf->nekf', d_recv, w_out, preferred_element_type=jnp.fl...  22.2 us
  transfers between devices with their start and end apart: 17, of which 10 were waited for; matrix products, arithmetic and copies ran while one was open for 25% of the time, Pallas kernels for 0%

profile of v1, /device:TPU:0, one launch (start us, length us, event | category | flops | bytes accessed | tf_op | source)
XLA Modules:
  0.0 868.0 jit_solution(8608930864037233032)
XLA Ops:
  14.5 11.6 %all-reduce.9 = (bf16[768]{0:T(1024)(128)(2,1)S(1)}, bf16[768]{0:T(1024)(128)(2,1)S(1)}) all-reduce(bf16[768]{0:T(1024)(128)(2,1)S(1)} %dynamic-update-slice, bf16[768]{0:T(1024)(128)(2,1)S(1)} %dynamic-update-slice.1), channel_id=1, replica_groups=mesh['dp'=4,'expert'=8] {'dp'}, use_global_device_ids=true, to_apply=%add.2 | all-reduce | flops 1536 | bytes 6144
  49.3 8.5 fusion.1
  66.9 15.8 %fusion.134 = (f32[12,512]{1,0:T(8,128)S(1)}, f32[12,512,512]{1,2,0:T(8,128)S(1)}) fusion(f32[512,512,12]{0,2,1:T(8,128)} %fusion.1, bf16[512,12,64]{0,2,1:T(8,128)(2,1)S(1)} %bitcast.277, bf16[512,12,64]{0,2,1:T(8,128)(2,1)S(1)} %bitcast.271, pred[512,512]{0,1:T(8,128)(4,1)S(1)} %fusion.94), kind=kOutput, calls=%fused_computation.211 | convolution fusion | flops 415229952 | bytes 27025408 | tf_op jit(solution)/shard_map/while/body/eval_jaxpr/qhd,khd->hqk/dot_general | solution.py:92
  110.1 8.1 all-gather.1
  134.9 30.0 %all-to-all-done = bf16[8,1,192,768]{3,2,1,0:T(8,128)(2,1)} async-done(((bf16[8,1,192,768]{3,2,1,0:T(8,128)(2,1)}), bf16[8,1,192,768]{3,2,1,0:T(8,128)(2,1)}, u32[]{:S(2)}, u32[]{:S(2)}) %all-to-all-start) | async-done | bytes 2359328 | tf_op jit(solution)/shard_map/all_to_all | solution.py:135
  169.4 13.8 %fusion.38 = f32[8,192,3072]{2,1,0:T(8,128)} fusion(bf16[1,768,3072]{2,1,0:T(8,128)(2,1)} %param.22, bf16[8,1,192,768]{3,2,1,0:T(8,128)(2,1)} %all-to-all-done), kind=kOutput, calls=%fused_computation.55 | convolution fusion | flops 7247757312 | bytes 25952256 | tf_op jit(solution)/shard_map/nekd,edf->nekf/dot_general | solution.py:136
  183.2 17.3 %convert_bitcast_fusion = bf16[8,1,192,768]{3,2,1,0:T(8,128)(2,1)} fusion(bf16[1,768,3072]{2,1,0:T(8,128)(2,1)} %param.23, f32[8,192,3072]{2,1,0:T(8,128)} %fusion.38), kind=kOutput, calls=%fused_computation.76 | convolution fusion | flops 7291404288 | bytes 25952256 | tf_op jit(solution)/shard_map/nekf,edf->nekd/dot_general | solution.py:138
  200.4 23.6 %all-to-all-done.2 = bf16[8,1,192,768]{3,2,1,0:T(8,128)(2,1)} async-done(((bf16[8,1,192,768]{3,2,1,0:T(8,128)(2,1)}), bf16[8,1,192,768]{3,2,1,0:T(8,128)(2,1)}, u32[]{:S(2)}, u32[]{:S(2)}) %all-to-all-start.2) | async-done | bytes 2359328 | tf_op jit(solution)/shard_map/all_to_all | solution.py:166
  228.5 22.2 %fusion.8 = bf16[8,1,192,3072]{3,2,0,1:T(8,128)(2,1)S(1)} fusion(f32[8,192,3072]{2,1,0:T(8,128)} %fusion.38, bf16[1,768,3072]{2,1,0:T(8,128)(2,1)} %param.23, bf16[8,1,192,768]{3,2,1,0:T(8,128)(2,1)} %all-to-all-done.2), kind=kOutput, calls=%fused_computation.19 | convolution fusion | flops 7342129152 | bytes 35389440 | tf_op jit(solution)/shard_map/nekd,edf->nekf/dot_general | solution.py:170
  250.7 13.5 %fusion.56 = bf16[8,192,768]{2,1,0:T(8,128)(2,1)S(1)} fusion(bf16[1,768,3072]{2,1,0:T(8,128)(2,1)} %param.22, bf16[8,1,192,3072]{3,2,0,1:T(8,128)(2,1)S(1)} %fusion.8), kind=kOutput, calls=%fused_computation.77 | convolution fusion | flops 7248936960 | bytes 16515072 | tf_op jit(solution)/shard_map/nekf,edf->nekd/dot_general | solution.py:176
  274.2 17.1 %collective-permute-done.1 = bf16[1,1,192,768]{3,2,1,0:T(8,128)(2,1)S(1)} collective-permute-done((bf16[1,1,192,768]{3,2,1,0:T(8,128)(2,1)S(1)}, bf16[1,1,192,768]{3,2,1,0:T(8,128)(2,1)S(1)}, u32[]{:S(2)}, u32[]{:S(2)}) %collective-permute-start.1) | collective-permute-done | bytes 294944 | tf_op jit(solution)/shard_map/ppermute | solution.py:184
  300.0 33.6 %collective-permute-done.3 = bf16[1,1,192,768]{3,2,1,0:T(8,128)(2,1)S(1)} collective-permute-done((bf16[1,1,192,768]{3,2,1,0:T(8,128)(2,1)S(1)}, bf16[1,1,192,768]{3,2,1,0:T(8,128)(2,1)S(1)}, u32[]{:S(2)}, u32[]{:S(2)}) %collective-permute-start.3) | collective-permute-done | bytes 294944 | tf_op jit(solution)/shard_map/ppermute | solution.py:184
  378.9 9.6 %multiply_reduce_fusion.1 = (f32[512,2]{1,0:T(8,128)}, f32[512,768]{1,0:T(8,128)}) fusion(f32[512,2,768]{2,1,0:T(2,128)} %reshape.582, f32[512,768]{1,0:T(8,128)S(1)} %convert_multiply_fusion.4, f32[512,2]{1,0:T(8,128)S(1)} %copy.124), kind=kLoop, calls=%fused_computation.61 | loop fusion | flops 2751488 | bytes 6299648 | tf_op jit(solution)/shard_map/reduce_sum | solution.py:156
  398.5 7.7 fusion.70
  406.2 7.7 multiply_reduce_fusion
  419.4 10.4 %fusion.74 = f32[12,32]{1,0:T(8,128)S(1)} fusion(s32[512,512]{0,1:T(8,128)} %copy-done.12, bf16[12,512,512]{1,2,0:T(8,128)(2,1)} %multiply_convert_fusion), kind=kOutput, calls=%fused_computation.101 | convolution fusion | flops 209715200 | bytes 7341568 | tf_op jit(solution)/shard_map/while/body/eval_jaxpr/hqk,qkb->hb/dot_general | solution.py:240
  444.9 188.6 %all-reduce.11 = (bf16[768,2304]{1,0:T(8,128)(2,1)}, bf16[768,768]{1,0:T(8,128)(2,1)}, bf16[768,8]{0,1:T(8,128)(2,1)S(1)}, bf16[768]{0:T(1024)(128)(2,1)S(1)}, b...) all-reduce(f32[768,2304]{1,0:T(8,128)} %fusion.95, ...), channel_id=1, replica_groups=mesh['dp'=4,'expert'=8] {'expert'}, use_global_device_ids=true, to_apply=%region_20.21 | all-reduce | flops 2367360 | bytes 14204160 | tf_op jit(solution)/shard_map/psum | solution.py:267
  635.0 14.4 %fusion.43 = bf16[1,768,3072]{2,1,0:T(8,128)(2,1)} fusion(f32[8,192,3072]{2,1,0:T(8,128)} %fusion.38, bf16[8,1,192,768]{3,2,1,0:T(8,128)(2,1)} %all-to-all-done.2), kind=kOutput, calls=%fused_computation.59 | convolution fusion | flops 7292583936 | bytes 25952256 | tf_op jit(solution)/shard_map/nekd,nekf->edf/dot_general | solution.py:172
  649.5 12.4 %fusion.40 = bf16[1,768,3072]{2,1,0:T(8,128)(2,1)} fusion(bf16[8,1,192,3072]{3,2,0,1:T(8,128)(2,1)} %copy-done.35, bf16[8,1,192,768]{3,2,1,0:T(8,128)(2,1)} %all-to-all-done), kind=kOutput, calls=%fused_computation.58 | convolution fusion | flops 7250116608 | bytes 16515072 | tf_op jit(solution)/shard_map/nekd,nekf->edf/dot_general | solution.py:175
  664.0 9.7 %all-reduce.8 = (bf16[768]{0:T(1024)(128)(2,1)S(1)}, bf16[768]{0:T(1024)(128)(2,1)S(1)}, bf16[12,32]{1,0:T(8,128)(2,1)S(1)}) all-reduce(bf16[768]{0:T(1024)(128)(2,1)S(1)} %get-tuple-element.77, bf16[768]{0:T(1024)(128)(2,1)S(1)} %get-tuple-element.78, ...), channel_id=5, replica_groups=mesh['dp'=4,'expert'=8] {'dp'}, use_global_device_ids=true, to_apply=%region_28.29.clone | all-reduce | flops 1920 | bytes 7680
  679.8 8.5 reduce-scatter.10.cloned.1.call-done
  690.1 58.0 %reduce-scatter.14.cloned.1.call-done = bf16[1,768,768]{2,1,0:T(8,128)(2,1)} async-done(((bf16[1,768,3072]{2,1,0:T(8,128)(2,1)}), bf16[1,768,768]{2,1,0:T(8,128)(2,1)}) %reduce-scatter.14.cloned.1.call-update) | async-done | bytes 1179664 | tf_op jit(solution)/shard_map/reduce_scatter | solution.py:191
  751.0 57.0 %reduce-scatter.12.cloned.1.call-done = bf16[1,768,768]{2,1,0:T(8,128)(2,1)} async-done(((bf16[1,768,3072]{2,1,0:T(8,128)(2,1)}), bf16[1,768,768]{2,1,0:T(8,128)(2,1)}) %reduce-scatter.12.cloned.1.call-update) | async-done | bytes 1179664 | tf_op jit(solution)/shard_map/reduce_scatter | solution.py:188
  810.8 47.4 %reduce-scatter.8.cloned.1.call-done = bf16[192,2304]{1,0:T(8,128)(2,1)} async-done(((bf16[768,2304]{1,0:T(8,128)(2,1)}), bf16[192,2304]{1,0:T(8,128)(2,1)}) %reduce-scatter.8.cloned.1.call-update) | async-done | bytes 884752 | tf_op jit(solution)/shard_map/reduce_scatter | solution.py:272
  (232 shorter events, 203.6 us)
Async XLA Ops:
  7.2 18.8 %copy-start.30 = (bf16[3,32]{1,0:T(4,128)(2,1)S(1)}, bf16[3,32]{1,0:T(4,128)(2,1)}, u32[]{:S(2)}) copy-start(bf16[3,32]{1,0:T(4,128)(2,1)} %param.21) | copy-start | bytes 580
  7.2 52.6 %all-gather.5.cloned.1.call-start = ((), (), s32[]{:S(2)}) async-start(), calls=%async_computation.8 | async-start | bytes 4423680 | tf_op jit(solution)/shard_map/all_gather | solution.py:50
  8.0 86.8 %all-gather.7.cloned.1.call-start = ((), (), s32[]{:S(2)}) async-start(), calls=%async_computation.9 | async-start | bytes 1474560 | tf_op jit(solution)/shard_map/all_gather | solution.py:51
  12.4 45.4 %copy-start.12 = (s32[512,512]{0,1:T(8,128)}, s32[512,512]{0,1:T(8,128)S(1)}, u32[]{:S(2)}) copy-start(s32[512,512]{0,1:T(8,128)S(1)} %compare_select_fusion) | copy-start | bytes 3145732
  12.7 20.7 %copy-start.22 = (f32[512]{0:T(512)}, f32[512]{0:T(512)S(1)}, u32[]{:S(2)}) copy-start(f32[512]{0:T(512)S(1)} %fusion.68) | copy-start | bytes 6148
  12.7 47.1 %copy-start.26 = (f32[512]{0:T(512)}, f32[512]{0:T(512)S(1)}, u32[]{:S(2)}) copy-start(f32[512]{0:T(512)S(1)} %fusion.116) | copy-start | bytes 6148
  26.0 33.8 %copy-start.24 = (f32[768]{0:T(1024)}, f32[768]{0:T(1024)S(1)}, u32[]{:S(2)}) copy-start(f32[768]{0:T(1024)S(1)} %convert_element_type.372) | copy-start | bytes 9220
  65.2 17.5 %copy-start.6 = (bf16[512,768]{0,1:T(8,128)(2,1)}, bf16[512,768]{0,1:T(8,128)(2,1)S(1)}, u32[]{:S(2)}) copy-start(bf16[512,768]{0,1:T(8,128)(2,1)S(1)} %copy.120) | copy-start | bytes 2359300
  66.9 15.8 %copy-start.10 = (bf16[512,768]{0,1:T(8,128)(2,1)}, bf16[512,768]{0,1:T(8,128)(2,1)S(1)}, u32[]{:S(2)}) copy-start(bf16[512,768]{0,1:T(8,128)(2,1)S(1)} %copy.119) | copy-start | bytes 2359300
  105.3 59.5 %all-to-all-start = ((bf16[8,1,192,768]{3,2,1,0:T(8,128)(2,1)}), bf16[8,1,192,768]{3,2,1,0:T(8,128)(2,1)}, u32[]{:S(2)}, u32[]{:S(2)}) async-start(bf16[8,1,192,768]{3,2,1,0:T(8,128)(2,1)} %broadcast_multiply_fusion), calls=%async_computation | async-start | bytes 4718592 | tf_op jit(solution)/shard_map/all_to_all | solution.py:135
  164.9 59.2 %all-to-all-start.2 = ((bf16[8,1,192,768]{3,2,1,0:T(8,128)(2,1)}), bf16[8,1,192,768]{3,2,1,0:T(8,128)(2,1)}, u32[]{:S(2)}, u32[]{:S(2)}) async-start(bf16[8,1,192,768]{3,2,1,0:T(8,128)(2,1)} %multiply_convert_fusion.1), calls=%async_computation.2 | async-start | bytes 4718592 | tf_op jit(solution)/shard_map/all_to_all | solution.py:166
  224.0 139.1 %all-to-all-start.1 = ((bf16[8,1,192,768]{3,2,1,0:T(8,128)(2,1)}), bf16[8,1,192,768]{3,2,1,0:T(8,128)(2,1)}, u32[]{:S(2)}, u32[]{:S(2)}) async-start(bf16[8,1,192,768]{3,2,1,0:T(8,128)(2,1)} %convert_bitcast_fusion), calls=%async_computation.1 | async-start | bytes 4718592 | tf_op jit(solution)/shard_map/all_to_all | solution.py:141
  228.4 449.9 %reduce-scatter.16.cloned.1.call-start = ((), (), s32[]{:S(2)}) async-start(), calls=%async_computation.14 | async-start | bytes 245760
  264.4 6.7 collective-permute-start
  264.8 26.5 %collective-permute-start.1 = (bf16[1,1,192,768]{3,2,1,0:T(8,128)(2,1)S(1)}, bf16[1,1,192,768]{3,2,1,0:T(8,128)(2,1)S(1)}, u32[]{:S(2)}, u32[]{:S(2)}) collective-permute-start(bf16[1,1,192,768]{3,2,1,0:T(8,128)(2,1)S(1)} %get-tuple-element.106), channel_id=1, source_target_pairs={{0,2},{1,3},{2,0},{3,1},{4,6},{5,7},{6,4},{7,5},{8,10},{9,11},{10,... | collective-permute-start | bytes 884744 | tf_op jit(solution)/shard_map/ppermute | solution.py:184
  267.2 68.6 %collective-permute-start.6 = (bf16[1,1,192,768]{3,2,0,1:T(8,128)(2,1)S(1)}, bf16[1,1,192,768]{3,2,0,1:T(8,128)(2,1)S(1)}, u32[]{:S(2)}, u32[]{:S(2)}) collective-permute-start(bf16[1,1,192,768]{3,2,0,1:T(8,128)(2,1)S(1)} %get-tuple-element.101), channel_id=1, source_target_pairs={{0,7},{1,6},{2,5},{3,4},{4,3},{5,2},{6,1},{7,0},{8,15},{9,14},{10,... | collective-permute-start | bytes 884744 | tf_op jit(solution)/shard_map/ppermute | solution.py:184
  269.3 65.8 %collective-permute-start.5 = (bf16[1,1,192,768]{3,2,1,0:T(8,128)(2,1)S(1)}, bf16[1,1,192,768]{3,2,1,0:T(8,128)(2,1)S(1)}, u32[]{:S(2)}, u32[]{:S(2)}) collective-permute-start(bf16[1,1,192,768]{3,2,1,0:T(8,128)(2,1)S(1)} %get-tuple-element.102), channel_id=1, source_target_pairs={{0,6},{1,7},{2,4},{3,5},{4,2},{5,3},{6,0},{7,1},{8,14},{9,15},{10,... | collective-permute-start | bytes 884744 | tf_op jit(solution)/shard_map/ppermute | solution.py:184
  270.8 63.6 %collective-permute-start.4 = (bf16[1,1,192,768]{3,2,1,0:T(8,128)(2,1)S(1)}, bf16[1,1,192,768]{3,2,1,0:T(8,128)(2,1)S(1)}, u32[]{:S(2)}, u32[]{:S(2)}) collective-permute-start(bf16[1,1,192,768]{3,2,1,0:T(8,128)(2,1)S(1)} %get-tuple-element.103), channel_id=1, source_target_pairs={{0,5},{1,4},{2,7},{3,6},{4,1},{5,0},{6,3},{7,2},{8,13},{9,12},{10,... | collective-permute-start | bytes 884744 | tf_op jit(solution)/shard_map/ppermute | solution.py:184
  271.1 28.2 %collective-permute-start.2 = (bf16[1,1,192,768]{3,2,1,0:T(8,128)(2,1)S(1)}, bf16[1,1,192,768]{3,2,1,0:T(8,128)(2,1)S(1)}, u32[]{:S(2)}, u32[]{:S(2)}) collective-permute-start(bf16[1,1,192,768]{3,2,1,0:T(8,128)(2,1)S(1)} %get-tuple-element.105), channel_id=1, source_target_pairs={{0,3},{1,2},{2,1},{3,0},{4,7},{5,6},{6,5},{7,4},{8,11},{9,10},{10,... | collective-permute-start | bytes 884744 | tf_op jit(solution)/shard_map/ppermute | solution.py:184
  291.2 42.4 %collective-permute-start.3 = (bf16[1,1,192,768]{3,2,1,0:T(8,128)(2,1)S(1)}, bf16[1,1,192,768]{3,2,1,0:T(8,128)(2,1)S(1)}, u32[]{:S(2)}, u32[]{:S(2)}) collective-permute-start(bf16[1,1,192,768]{3,2,1,0:T(8,128)(2,1)S(1)} %get-tuple-element.104), channel_id=1, source_target_pairs={{0,4},{1,5},{2,6},{3,7},{4,0},{5,1},{6,2},{7,3},{8,12},{9,13},{10,... | collective-permute-start | bytes 884744 | tf_op jit(solution)/shard_map/ppermute | solution.py:184
  634.4 53.9 %reduce-scatter.10.cloned.1.call-start = ((), (), s32[]{:S(2)}) async-start(), calls=%async_computation.11 | async-start | bytes 1474560 | tf_op jit(solution)/shard_map/reduce_scatter | solution.py:275
  634.9 113.2 %reduce-scatter.14.cloned.1.call-start = ((), (), s32[]{:S(2)}) async-start(), calls=%async_computation.13 | async-start | bytes 5898240 | tf_op jit(solution)/shard_map/reduce_scatter | solution.py:191
  649.4 158.5 %reduce-scatter.12.cloned.1.call-start = ((), (), s32[]{:S(2)}) async-start(), calls=%async_computation.12 | async-start | bytes 5898240 | tf_op jit(solution)/shard_map/reduce_scatter | solution.py:188
  662.0 196.3 %reduce-scatter.8.cloned.1.call-start = ((), (), s32[]{:S(2)}) async-start(), calls=%async_computation.10 | async-start | bytes 4423680 | tf_op jit(solution)/shard_map/reduce_scatter | solution.py:272
  (32 other events, 189.9 us)
Sparse Core Ops, SparseCore 0:
  9.9 49.8 all-gather.4
  61.6 27.5 all-gather.6
  634.5 21.6 reduce-scatter.15
  659.5 28.6 reduce-scatter.9
  691.1 56.9 reduce-scatter.13
  751.0 56.9 reduce-scatter.11
  811.0 47.1 reduce-scatter.7
